TPU v7x, 64 devices: a 2x2x8 block of a 4x4x8 slice. The times are simulated.
64 devices in a mesh: batch: 4 (over x, y), col: 16 (over z, core).
Axes of the slice: x: 2, y: 2, z: 8, core: 2. Of those that a mesh axis runs over, the one named last changes fastest.
The devices are a block of a 4x4x8 slice.
Arguments:
- lower: bfloat16 [16384, 4096], P('batch', 'col'), parts along dimension 0
- rhs: bfloat16 [16384, 16384], P('batch', 'col'), parts along dimension 0
Outputs:
- output: bfloat16 [16384, 16384], P('batch', 'col'), parts along dimension 0
There are 4 independent parts. A program takes and returns all parts, laid end to end along the dimension named above; each array names one.
All inputs are finite; a program needn't handle non-finite values.
Results may differ from a plain program's by a relative error of at most 0.001.
Values are sent between devices in bfloat16 or wider.
A program may use at most 768 MiB of HBM per device.

v0:
```python
import jax
import jax.numpy as jnp
from jax import lax
from jax.sharding import PartitionSpec as P

BLOCK_SIZE = 256


def solution(mesh):
    group_size = mesh.shape["col"]

    def local_product(l_cols, b_cols):
        mat_order, local_width = l_cols.shape
        per_dev = local_width // BLOCK_SIZE
        super_width = group_size * BLOCK_SIZE
        pieces = [l_cols[panel_idx * super_width:, panel_idx * BLOCK_SIZE:(panel_idx + 1) * BLOCK_SIZE] for panel_idx in range(per_dev)]
        packed = jnp.concatenate(pieces, axis=0)
        gathered = lax.all_gather(packed, "col")
        col_bands = []
        offset = 0
        for panel_idx in range(per_dev):
            band_rows = mat_order - panel_idx * super_width
            panel_band = gathered[:, offset:offset + band_rows, :]
            offset = offset + band_rows
            panel_band = jnp.transpose(panel_band, (1, 0, 2)).reshape(band_rows, super_width)
            col_bands.append(jnp.pad(panel_band, ((panel_idx * super_width, 0), (0, 0))))
        natural = jnp.concatenate(col_bands, axis=1)
        out_rows = []
        for row_idx in range(mat_order // BLOCK_SIZE):
            row_end = (row_idx + 1) * BLOCK_SIZE
            strip = natural[row_idx * BLOCK_SIZE:row_end, :row_end]
            block_out = jnp.dot(strip, b_cols[:row_end], preferred_element_type=jnp.float32)
            out_rows.append(block_out.astype(jnp.bfloat16))
        return jnp.concatenate(out_rows, axis=0)

    return jax.shard_map(local_product, mesh=mesh, in_specs=(P("batch", "col"), P("batch", "col")), out_specs=P("batch", "col"), check_vma=False)
```

profile of v0, /device:TPU:22, one launch (start us, length us, event | category | flops | bytes accessed | tf_op | source)
XLA Modules:
  0.0 284.6 jit_solution(677903629280646857)
XLA Ops:
  6.5 0.0 all-gather.3.cloned.1.call-start
  6.6 0.7 all-gather.3.cloned.1.call-update
  7.3 176.4 %all-gather.3.cloned.1.call-done = bf16[65536,256]{1,0:T(8,128)(2,1)} async-done(((bf16[4096,256]{1,0:T(8,128)(2,1)}), bf16[65536,256]{1,0:T(8,128)(2,1)}) %all-gather.3.cloned.1.call-update) | async-done | bytes 33554448 | tf_op jit(solution)/shard_map/all_gather | solution.py:18
  183.7 3.1 %slice.143 = bf16[256,16,256]{2,0,1:T(8,128)(2,1)} slice(bf16[4096,16,256]{2,0,1:T(8,128)(2,1)} %bitcast.7), slice={[3840:4096], [0:16], [0:256]} | slice | bytes 4194304 | tf_op jit(solution)/shard_map/slice | solution.py:31
  186.8 40.5 %copy.3 = bf16[4096,16,256]{0,2,1:T(8,128)(2,1)} copy(bf16[4096,16,256]{2,0,1:T(8,128)(2,1)} %bitcast.8) | data formatting | bytes 67108864 | tf_op jit(solution)/shard_map/transpose | solution.py:25
  227.4 2.8 %copy.4 = bf16[256,16,256]{0,2,1:T(8,128)(2,1)S(1)} copy(bf16[256,16,256]{2,0,1:T(8,128)(2,1)} %slice.143) | data formatting | bytes 4194304 | tf_op jit(solution)/shard_map/slice | solution.py:31
  230.2 0.0 slice-start
  230.2 1.6 fusion.74
  231.8 1.8 fusion.67
  233.6 2.2 fusion.78
  235.8 0.0 slice-start.1
  235.8 2.6 fusion.71
  238.4 2.8 fusion.92
  241.3 0.0 slice-done
  241.3 0.0 slice-done.1
  241.3 2.1 fusion.123
  243.4 2.3 fusion.134
  245.8 2.5 fusion.131
  248.3 2.7 fusion.120
  251.0 2.9 %fusion.115 = bf16[4096,1024]{1,0:T(8,128)(2,1)S(1)} fusion(bf16[4096,1024]{1,0:T(8,128)(2,1)S(1)} %fusion.120, bf16[4096,1024]{1,0:T(8,128)(2,1)S(1)} %bitcast.25, bf16[4096,4096]{0,1:T(8,128)(2,1)} %bitcast.18), kind=kOutput, calls=%fused_computation.58 | convolution fusion | flops 1342439424 | bytes 7077888 | tf_op jit(solution)/shard_map/dot_general | solution.py:32
  253.8 3.1 %fusion.126 = bf16[4096,1024]{1,0:T(8,128)(2,1)S(1)} fusion(bf16[4096,1024]{1,0:T(8,128)(2,1)S(1)} %fusion.115, bf16[4096,1024]{1,0:T(8,128)(2,1)S(1)} %bitcast.25, bf16[4096,4096]{0,1:T(8,128)(2,1)} %bitcast.19), kind=kOutput, calls=%fused_computation.61 | convolution fusion | flops 1476657152 | bytes 7733248 | tf_op jit(solution)/shard_map/dot_general | solution.py:32
  256.9 3.2 %fusion.110 = bf16[4096,1024]{1,0:T(8,128)(2,1)S(1)} fusion(bf16[4096,1024]{1,0:T(8,128)(2,1)S(1)} %fusion.126, bf16[4096,1024]{1,0:T(8,128)(2,1)S(1)} %bitcast.25, bf16[4096,4096]{0,1:T(8,128)(2,1)} %bitcast.20), kind=kOutput, calls=%fused_computation.57 | convolution fusion | flops 1610874880 | bytes 8388608 | tf_op jit(solution)/shard_map/dot_general | solution.py:32
  260.1 3.4 %fusion.105 = bf16[4096,1024]{1,0:T(8,128)(2,1)S(1)} fusion(bf16[4096,1024]{1,0:T(8,128)(2,1)S(1)} %fusion.110, bf16[4096,1024]{1,0:T(8,128)(2,1)S(1)} %bitcast.25, bf16[4096,4096]{0,1:T(8,128)(2,1)} %bitcast.21), kind=kOutput, calls=%fused_computation.56 | convolution fusion | flops 1745092608 | bytes 9043968 | tf_op jit(solution)/shard_map/dot_general | solution.py:32
  263.6 3.8 %fusion.100 = bf16[4096,1024]{1,0:T(8,128)(2,1)S(1)} fusion(bf16[4096,1024]{1,0:T(8,128)(2,1)S(1)} %fusion.105, bf16[4096,1024]{1,0:T(8,128)(2,1)S(1)} %bitcast.25, bf16[4096,4096]{0,1:T(8,128)(2,1)} %bitcast.22), kind=kOutput, calls=%fused_computation.55 | convolution fusion | flops 1879310336 | bytes 9699328 | tf_op jit(solution)/shard_map/dot_general | solution.py:32
  267.4 3.8 %fusion.95 = bf16[4096,1024]{1,0:T(8,128)(2,1)S(1)} fusion(bf16[4096,1024]{1,0:T(8,128)(2,1)S(1)} %fusion.100, bf16[4096,1024]{1,0:T(8,128)(2,1)S(1)} %bitcast.25, bf16[4096,4096]{0,1:T(8,128)(2,1)} %bitcast.23), kind=kOutput, calls=%fused_computation.54 | convolution fusion | flops 2013528064 | bytes 10354688 | tf_op jit(solution)/shard_map/dot_general | solution.py:32
  271.2 0.0 copy-start
  271.2 3.4 %copy-done = bf16[4096,1024]{1,0:T(8,128)(2,1)} copy-done((bf16[4096,1024]{1,0:T(8,128)(2,1)}, bf16[4096,1024]{1,0:T(8,128)(2,1)S(1)}, u32[]{:S(2)}) %copy-start) | copy-done | bytes 8388632
  274.6 3.2 %fusion.66 = bf16[4096,1024]{1,0:T(8,128)(2,1)} fusion(bf16[4096,1024]{1,0:T(8,128)(2,1)} %copy-done, bf16[256,4096]{0,1:T(8,128)(2,1)S(1)} %bitcast.26, bf16[4096,1024]{1,0:T(8,128)(2,1)S(1)} %bitcast.25), kind=kOutput, calls=%fused_computation.41 | convolution fusion | flops 2147745792 | bytes 11010048 | tf_op jit(solution)/shard_map/dot_general | solution.py:32
  (1 shorter events, 0.0 us)
Async XLA Ops:
  6.5 177.2 %all-gather.3.cloned.1.call-start = ((), (), s32[]{:S(2)}) async-start(), calls=%async_computation | async-start | bytes 35651584 | tf_op jit(solution)/shard_map/all_gather | solution.py:18
  230.2 11.0 %slice-start = ((s8[8388608]{0:T(1024)(128)(4,1)}), s8[4194304]{0:T(1024)(128)(4,1)S(1)}, s32[]{:S(2)}) async-start(s8[8388608]{0:T(1024)(128)(4,1)} %bitcast.24), calls=%async_computation.1 | async-start | bytes 8388608
  235.8 5.5 %slice-start.1 = ((s8[8388608]{0:T(1024)(128)(4,1)}), s8[4194304]{0:T(1024)(128)(4,1)S(1)}, s32[]{:S(2)}) async-start(s8[8388608]{0:T(1024)(128)(4,1)} %bitcast.24), calls=%async_computation.2 | async-start | bytes 8388608
  271.2 3.4 %copy-start = (bf16[4096,1024]{1,0:T(8,128)(2,1)}, bf16[4096,1024]{1,0:T(8,128)(2,1)S(1)}, u32[]{:S(2)}) copy-start(bf16[4096,1024]{1,0:T(8,128)(2,1)S(1)} %fusion.95) | copy-start | bytes 25165828
Sparse Core Ops, SparseCore 0:
  9.0 174.7 all-gather.2
where the time goes:
time: 288 us; the launch traced here: 285 us
  waiting for transfers between devices  177 us (61%)
  local copies, waits for them, and re-layouts  49.9 us (17%)
  matrix products  44 us (15%)
  between operations  13.6 us (5%)
    all_gather x1, waiting for transfers between devices, local_product(): gathered = lax.all_gather(packed, 'col')  176 us
    dot_general x16, matrix products, local_product(): jnp.dot(strip, b_cols[:row_end], preferred_element_type=jnp.float32)  44 us
    transpose x1, local copies, waits for them, and re-layouts, local_product(): jnp.transpose(panel_band, (1, 0, 2)).reshape(band_rows, super_width)  40.5 us
    slice x2, local copies, waits for them, and re-layouts, local_product(): strip = natural[row_idx * BLOCK_SIZE:row_end, :row_end]  5.94 us
  transfers between devices with their start and end apart: 1, of which 1 were waited for; matrix products, arithmetic and copies ran while one was open for 0% of the time, Pallas kernels for 0%

commit v1 on v0

v1 whole, which is shorter than its diff:
```python
import functools

import jax
import jax.numpy as jnp
from jax import lax
from jax.experimental import pallas as pl
from jax.experimental.pallas import tpu as pltpu
from jax.sharding import PartitionSpec as P

BLOCK = 256
MESH = pl.DeviceIdType.MESH
CHIPS = 8
PLUS_HOPS = (2, 2, 3, 5, 4, 4, 3, 2)
LONGER = {(0, 3): 12, (1, 3): 7, (1, 4): 13, (2, 4): 6, (2, 5): 9}
MORE_ODD = (2, 5)


def pick(index, values):
    out = jnp.int32(values[-1])
    for j in range(len(values) - 2, -1, -1):
        out = jnp.where(index == j, jnp.int32(values[j]), out)
    return out


def kernel(nb, l_ref, b_ref, acc, lv, bv, rsem, psem, msem, dsem, bsem):
    c = lax.axis_index("col")
    z, p = c // 2, c % 2
    q = 1 - p
    nxt = ((z + 1) % CHIPS) * 2 + p
    prv = ((z + CHIPS - 1) % CHIPS) * 2 + p
    mate = z * 2 + q

    def split(s, d, par):
        t = jnp.where(d <= pick(s, PLUS_HOPS), 0, nb)
        for (s0, d0), v in LONGER.items():
            v = v - par if (s0, d0) == MORE_ODD else v
            t = jnp.where(s * CHIPS + d == s0 * CHIPS + d0, v, t)
        return t

    def slot(k, i):
        return nb * k - k * (k - 1) // 2 + i - k

    def remote(src, t, sem, dev):
        return pltpu.make_async_remote_copy(
            src_ref=src, dst_ref=lv.at[t], send_sem=sem, recv_sem=rsem.at[t],
            device_id={"col": dev}, device_id_type=MESH)

    def own_rows(i):
        return l_ref.at[pl.ds(pl.multiple_of(i * BLOCK, BLOCK), BLOCK), :]

    def b_copy(k):
        rows = pl.ds(pl.multiple_of(k * BLOCK, BLOCK), BLOCK)
        return pltpu.make_async_copy(b_ref.at[rows, :], bv.at[rows, :], bsem.at[k])

    def land(t):
        remote(lv.at[t], t, psem.at[t], nxt).wait_recv()

    def plus_start(d, par):
        s = (z + CHIPS - d) % CHIPS
        return jnp.maximum(2 * s + par, split(s, d, par))

    def plus_next(d, i, par):
        more = i < nb - 1
        d2 = d + 1
        i2 = jnp.where(more, i + 1, plus_start(d2, par))
        ended = i >= nb
        return jnp.where(more | ended, d, d2), jnp.where(ended, i, i2)

    def minus_start(d, par):
        s = (z + d) % CHIPS
        k = 2 * s + par
        return jnp.where(split(s, CHIPS - d, par) > k, k, nb)

    def minus_next(d, i, par):
        s = (z + d) % CHIPS
        more = i + 1 < split(s, CHIPS - d, par)
        d2 = d + 1
        i2 = jnp.where(more, i + 1, minus_start(d2, par))
        ended = i >= nb
        return jnp.where(more | ended, d, d2), jnp.where(ended, i, i2)

    barrier = pltpu.get_barrier_semaphore()
    for dev in (nxt, prv, mate):
        pl.semaphore_signal(barrier, inc=1, device_id={"col": dev}, device_id_type=MESH)
    pl.semaphore_wait(barrier, 3)

    def send_own(i, carry):
        t = slot(c, i)
        remote(own_rows(i), t, psem.at[t], nxt).start()
        remote(own_rows(i), t, msem.at[t], prv).start()
        remote(own_rows(i), t, dsem.at[t], mate).start()
        pltpu.make_async_copy(own_rows(i), lv.at[t], rsem.at[t]).start()
        return carry

    lax.fori_loop(c, nb, send_own, 0)

    def load_b(k, carry):
        b_copy(k).start()
        return carry

    lax.fori_loop(0, nb, load_b, 0)

    def clear(i, carry):
        acc[pl.ds(pl.multiple_of(i * 64, 64), 64), :] = jnp.zeros((64, acc.shape[1]), jnp.float32)
        return carry

    lax.fori_loop(0, acc.shape[0] // 64, clear, 0)

    def wait_b(k, carry):
        b_copy(k).wait()
        return carry

    lax.fori_loop(0, nb, wait_b, 0)

    def multiply(k, i):
        t = slot(k, i)
        rows = pl.ds(pl.multiple_of(i * BLOCK, BLOCK), BLOCK)
        depth = pl.ds(pl.multiple_of(k * BLOCK, BLOCK), BLOCK)
        tile = lv[t]
        half = acc.shape[1] // 2
        for n in range(2):
            cols = slice(n * half, (n + 1) * half)
            acc[rows, cols] += jnp.dot(tile, bv[depth, cols], preferred_element_type=jnp.float32)

    slots = 36

    def step(n, cur):
        pd, pi, md, mi, qpd, qpi, qmd, qmi = cur
        ps, ms = (z + CHIPS - pd) % CHIPS, (z + md) % CHIPS
        pk, mk = 2 * ps + p, 2 * ms + p

        @pl.when(pi < nb)
        def _():
            t = slot(pk, pi)
            land(t)

            @pl.when(split(ps, pd + 1, p) <= pi)
            def _():
                remote(lv.at[t], t, psem.at[t], nxt).start()

            remote(lv.at[t], t, dsem.at[t], mate).start()

        @pl.when(mi < nb)
        def _():
            t = slot(mk, mi)
            land(t)

            @pl.when(split(ms, CHIPS - 1 - md, p) > mi)
            def _():
                remote(lv.at[t], t, msem.at[t], prv).start()

            remote(lv.at[t], t, dsem.at[t], mate).start()

        qps, qms = (z + CHIPS - qpd) % CHIPS, (z + qmd) % CHIPS
        late = n >= 1
        own = c + n
        other = mate + n
        ks = (pk, mk, 2 * qps + q, 2 * qms + q, c, mate)
        is_ = (pi, mi, jnp.where(late, qpi, nb), jnp.where(late, qmi, nb), own, other)

        def one(j, carry):
            k, i = ks[-1], is_[-1]
            for x in range(4, -1, -1):
                k = jnp.where(j == x, ks[x], k)
                i = jnp.where(j == x, is_[x], i)

            @pl.when(i < nb)
            def _():
                @pl.when(j >= 2)
                def _():
                    land(slot(k, i))

                multiply(k, i)

            return carry

        lax.fori_loop(0, 6, one, 0)

        npd, npi = plus_next(pd, pi, p)
        nmd, nmi = minus_next(md, mi, p)
        a, b = plus_next(qpd, qpi, q)
        e, f = minus_next(qmd, qmi, q)
        hold = lambda new, old: jnp.where(late, new, old)
        return npd, npi, nmd, nmi, hold(a, qpd), hold(b, qpi), hold(e, qmd), hold(f, qmi)

    one_ = jnp.int32(1)
    lax.fori_loop(0, slots + 1, step, (
        one_, plus_start(1, p), one_, minus_start(1, p),
        one_, plus_start(1, q), one_, minus_start(1, q)))

    def sent_own(i, carry):
        t = slot(c, i)
        remote(own_rows(i), t, psem.at[t], nxt).wait_send()
        remote(own_rows(i), t, msem.at[t], prv).wait_send()
        remote(own_rows(i), t, dsem.at[t], mate).wait_send()
        return carry

    lax.fori_loop(c, nb, sent_own, 0)

    for d in range(1, CHIPS - 1):
        s = (z + CHIPS - d) % CHIPS
        k = 2 * s + p

        def sent_plus(i, carry):
            t = slot(k, i)
            remote(lv.at[t], t, psem.at[t], nxt).wait_send()
            return carry

        lax.fori_loop(jnp.maximum(k, split(s, d + 1, p)), nb, sent_plus, 0)

        def sent_plus_mate(i, carry):
            t = slot(k, i)
            remote(lv.at[t], t, dsem.at[t], mate).wait_send()
            return carry

        lax.fori_loop(jnp.maximum(k, split(s, d, p)), nb, sent_plus_mate, 0)

        s2 = (z + d) % CHIPS
        k2 = 2 * s2 + p

        def sent_minus(i, carry):
            t = slot(k2, i)
            remote(lv.at[t], t, msem.at[t], prv).wait_send()
            return carry

        lax.fori_loop(k2, split(s2, CHIPS - 1 - d, p), sent_minus, 0)

        def sent_minus_mate(i, carry):
            t = slot(k2, i)
            remote(lv.at[t], t, dsem.at[t], mate).wait_send()
            return carry

        lax.fori_loop(k2, split(s2, CHIPS - d, p), sent_minus_mate, 0)


def solution(mesh):
    def local(l_cols, b_cols):
        order, width = b_cols.shape
        nb = order // BLOCK
        tiles = nb * (nb + 1) // 2
        acc = pl.pallas_call(
            functools.partial(kernel, nb),
            out_shape=pltpu.VMEM((order, width), jnp.float32),
            in_specs=[pl.BlockSpec(memory_space=pltpu.HBM)] * 2,
            out_specs=pl.BlockSpec(memory_space=pltpu.VMEM),
            scratch_shapes=[
                pltpu.VMEM((tiles, BLOCK, BLOCK), jnp.bfloat16),
                pltpu.VMEM((order, width), jnp.bfloat16),
                pltpu.SemaphoreType.DMA((tiles,)),
                pltpu.SemaphoreType.DMA((tiles,)),
                pltpu.SemaphoreType.DMA((tiles,)),
                pltpu.SemaphoreType.DMA((tiles,)),
                pltpu.SemaphoreType.DMA((nb,)),
            ],
            compiler_params=pltpu.CompilerParams(
                collective_id=0, has_side_effects=True, vmem_limit_bytes=34 * 2**20),
        )(l_cols, b_cols)
        return acc.astype(jnp.bfloat16)

    return jax.shard_map(local, mesh=mesh, in_specs=(P("batch", "col"), P("batch", "col")),
                         out_specs=P("batch", "col"), check_vma=False)
```

time: 288 us -> 116 us (0.40)
  the two profiles are of different devices: /device:TPU:22 before, /device:TPU:247 now
where the time goes in v1:
time: 116 us
  Pallas kernels  110 us (95%)
  other arithmetic  4.02 us (3%)
  local copies, waits for them, and re-layouts  1.59 us (1%)
    pallas_call x1, Pallas kernels, local(): pl.pallas_call(functools.partial(kernel, nb), out_shape=pltpu.VMEM((order...  110 us
    convert_element_type x1, other arithmetic, local(): return acc.astype(jnp.bfloat16)  4.02 us

profile of v1, /device:TPU:247, one launch (start us, length us, event | category | flops | bytes accessed | tf_op | source)
XLA Modules:
  0.0 115.8 jit_solution(18169380392330636615)
XLA Ops:
  0.0 0.0 copy-start
  0.0 1.6 %copy-done = bf16[4096,256]{1,0:T(8,128)(2,1)S(1)} copy-done((bf16[4096,256]{1,0:T(8,128)(2,1)S(1)}, bf16[4096,256]{1,0:T(8,128)(2,1)}, u32[]{:S(2)}) %copy-start) | copy-done | bytes 2097176
  1.6 110.2 %shard_map.28 = f32[4096,1024]{1,0:T(8,128)S(1)} custom-call(bf16[4096,256]{1,0:T(8,128)(2,1)S(1)} %copy-done, bf16[4096,1024]{1,0:T(8,128)(2,1)} %b_ref.1), custom_call_target="tpu_custom_call" | custom-call | tf_op jit(solution)/shard_map/pallas_call | solution.py:241
  111.8 4.0 %convert_element_type.3 = bf16[4096,1024]{1,0:T(8,128)(2,1)} convert(f32[4096,1024]{1,0:T(8,128)S(1)} %shard_map.28) | non-fusion elementwise | flops 4194304 | bytes 25165824 | tf_op jit(solution)/shard_map/convert_element_type | solution.py:258
Async XLA Ops:
  0.0 1.6 %copy-start = (bf16[4096,256]{1,0:T(8,128)(2,1)S(1)}, bf16[4096,256]{1,0:T(8,128)(2,1)}, u32[]{:S(2)}) copy-start(bf16[4096,256]{1,0:T(8,128)(2,1)} %l_ref.1) | copy-start | bytes 6291460

commit v2 on v1

v2 whole, which is shorter than its diff:
```python
import functools

import jax
import jax.numpy as jnp
from jax import lax
from jax.experimental import pallas as pl
from jax.experimental.pallas import tpu as pltpu
from jax.sharding import PartitionSpec as P

BLOCK = 256
MESH = pl.DeviceIdType.MESH
CHIPS = 8
PLUS_HOPS = (2, 2, 3, 5, 4, 4, 3, 2)
LONGER = {(0, 3): 12, (1, 3): 7, (1, 4): 13, (2, 4): 6, (2, 5): 9}
MORE_ODD = (2, 5)
SLOTS = 36
OWN_SENT = 20


def pick(index, values):
    out = jnp.int32(values[-1])
    for j in range(len(values) - 2, -1, -1):
        out = jnp.where(index == j, jnp.int32(values[j]), out)
    return out


def kernel(nb, l_ref, b_ref, acc, lv, dg, bv, rsem, psem, msem, dsem, bsem):
    c = lax.axis_index("col")
    z, p = c // 2, c % 2
    q = 1 - p
    nxt = ((z + 1) % CHIPS) * 2 + p
    prv = ((z + CHIPS - 1) % CHIPS) * 2 + p
    mate = z * 2 + q
    half = BLOCK // 2

    def split(s, d, par):
        t = jnp.where(d <= pick(s, PLUS_HOPS), 0, nb)
        for (s0, d0), v in LONGER.items():
            v = v - par if (s0, d0) == MORE_ODD else v
            t = jnp.where(s * CHIPS + d == s0 * CHIPS + d0, v, t)
        return t

    def slot(k, i):
        return nb * k - k * (k - 1) // 2 + i - k

    def each(k, i, fn):
        t = slot(k, i)

        @pl.when(i == k)
        def _():
            fn(dg.at[k], t)

        @pl.when(i != k)
        def _():
            fn(lv.at[t], t)

    def remote(ref, t, sem, dev):
        return pltpu.make_async_remote_copy(
            src_ref=ref, dst_ref=ref, send_sem=sem.at[t], recv_sem=rsem.at[t],
            device_id={"col": dev}, device_id_type=MESH)

    def send(k, i, *ways):
        def go(ref, t):
            for sem, dev in ways:
                remote(ref, t, sem, dev).start()
        each(k, i, go)

    def sent(k, i, *ways):
        def go(ref, t):
            for sem, dev in ways:
                remote(ref, t, sem, dev).wait_send()
        each(k, i, go)

    def land(k, i):
        each(k, i, lambda ref, t: remote(ref, t, psem, nxt).wait_recv())

    def b_copy(k):
        rows = pl.ds(pl.multiple_of(k * BLOCK, BLOCK), BLOCK)
        return pltpu.make_async_copy(b_ref.at[rows, :], bv.at[rows, :], bsem.at[k])

    def plus_low(d, par):
        s = (z + CHIPS - d) % CHIPS
        return jnp.maximum(2 * s + par, split(s, d, par))

    def plus_start(d, par):
        return jnp.where(plus_low(d, par) < nb, nb - 1, -1)

    def plus_next(d, i, par):
        more = i > plus_low(d, par)
        ended = i < 0
        i2 = jnp.where(more, i - 1, plus_start(d + 1, par))
        return jnp.where(more | ended, d, d + 1), jnp.where(ended, i, i2)

    def minus_start(d, par):
        s = (z + d) % CHIPS
        k = 2 * s + par
        return jnp.where(split(s, CHIPS - d, par) > k, k, -1)

    def minus_next(d, i, par):
        s = (z + d) % CHIPS
        more = i + 1 < split(s, CHIPS - d, par)
        ended = i < 0
        i2 = jnp.where(more, i + 1, minus_start(d + 1, par))
        return jnp.where(more | ended, d, d + 1), jnp.where(ended, i, i2)

    def plus_block(d, par):
        return 2 * ((z + CHIPS - d) % CHIPS) + par

    def minus_block(d, par):
        return 2 * ((z + d) % CHIPS) + par

    def plus_onward(d, i):
        return (i >= 0) & (split((z + CHIPS - d) % CHIPS, d + 1, p) <= i)

    def minus_onward(d, i):
        return (i >= 0) & (split((z + d) % CHIPS, CHIPS - 1 - d, p) > i)

    barrier = pltpu.get_barrier_semaphore()
    for dev in (nxt, prv, mate):
        pl.semaphore_signal(barrier, inc=1, device_id={"col": dev}, device_id_type=MESH)

    diag_row = pl.multiple_of(c * BLOCK, BLOCK)
    t_diag = slot(c, c)
    pltpu.make_async_copy(
        l_ref.at[pl.ds(diag_row, BLOCK), pl.ds(0, half)],
        dg.at[c, pl.ds(0, BLOCK), :], rsem.at[t_diag]).start()
    pltpu.make_async_copy(
        l_ref.at[pl.ds(diag_row + half, half), pl.ds(half, half)],
        dg.at[c, pl.ds(BLOCK, half), :], rsem.at[t_diag]).start()

    def own_copy(i):
        rows = pl.ds(pl.multiple_of(i * BLOCK, BLOCK), BLOCK)
        t = slot(c, i)
        return pltpu.make_async_copy(l_ref.at[rows, :], lv.at[t], rsem.at[t])

    lax.fori_loop(c + 1, nb, lambda i, x: (own_copy(i).start(), x)[1], 0)
    lax.fori_loop(0, nb, lambda k, x: (b_copy(k).start(), x)[1], 0)
    lax.fori_loop(c, nb, lambda i, x: (land(c, i), x)[1], 0)
    pl.semaphore_wait(barrier, 3)

    def send_own(j, carry):
        send(c, nb - 1 - j, (psem, nxt))
        send(c, c + j, (msem, prv), (dsem, mate))
        return carry

    lax.fori_loop(0, nb - c, send_own, 0)

    def clear(i, carry):
        acc[pl.ds(pl.multiple_of(i * 64, 64), 64), :] = jnp.zeros((64, acc.shape[1]), jnp.float32)
        return carry

    lax.fori_loop(0, acc.shape[0] // 64, clear, 0)
    lax.fori_loop(0, nb, lambda k, x: (b_copy(k).wait(), x)[1], 0)

    width = acc.shape[1] // 2

    def multiply(k, i):
        row = pl.multiple_of(i * BLOCK, BLOCK)
        depth = pl.multiple_of(k * BLOCK, BLOCK)

        @pl.when(i != k)
        def _():
            tile = lv[slot(k, i)]
            for n in range(2):
                cols = slice(n * width, (n + 1) * width)
                acc[pl.ds(row, BLOCK), cols] += jnp.dot(
                    tile, bv[pl.ds(depth, BLOCK), cols], preferred_element_type=jnp.float32)

        @pl.when(i == k)
        def _():
            left, corner = dg[k, :BLOCK, :], dg[k, BLOCK:, :]
            for n in range(2):
                cols = slice(n * width, (n + 1) * width)
                acc[pl.ds(row, BLOCK), cols] += jnp.dot(
                    left, bv[pl.ds(depth, half), cols], preferred_element_type=jnp.float32)
                acc[pl.ds(row + half, half), cols] += jnp.dot(
                    corner, bv[pl.ds(depth + half, half), cols], preferred_element_type=jnp.float32)

    lag = nb - c + 3

    def left_onward(cur):
        pd, pi, md, mi = cur

        @pl.when(plus_onward(pd, pi))
        def _():
            sent(plus_block(pd, p), pi, (psem, nxt))

        @pl.when(minus_onward(md, mi))
        def _():
            sent(minus_block(md, p), mi, (msem, prv))

        return (*plus_next(pd, pi, p), *minus_next(md, mi, p))

    def step(n, cur):
        pd, pi, md, mi, qpd, qpi, qmd, qmi, *old = cur
        pk, mk = plus_block(pd, p), minus_block(md, p)

        @pl.when(pi >= 0)
        def _():
            land(pk, pi)

            @pl.when(plus_onward(pd, pi))
            def _():
                send(pk, pi, (psem, nxt))

            send(pk, pi, (dsem, mate))

        @pl.when(mi >= 0)
        def _():
            land(mk, mi)

            @pl.when(minus_onward(md, mi))
            def _():
                send(mk, mi, (msem, prv))

            send(mk, mi, (dsem, mate))

        late = n >= 1
        own = jnp.where(c + n < nb, c + n, -1)
        other = jnp.where(mate + n < nb, mate + n, -1)
        ks = (pk, mk, c, plus_block(qpd, q), minus_block(qmd, q), mate)
        is_ = (pi, mi, own, jnp.where(late, qpi, -1), jnp.where(late, qmi, -1), other)

        def one(j, carry):
            k, i = ks[-1], is_[-1]
            for x in range(4, -1, -1):
                k = jnp.where(j == x, ks[x], k)
                i = jnp.where(j == x, is_[x], i)

            @pl.when(i >= 0)
            def _():
                @pl.when(j >= 3)
                def _():
                    land(k, i)

                multiply(k, i)

                @pl.when(j < 3)
                def _():
                    sent(k, i, (dsem, mate))

            return carry

        lax.fori_loop(0, 6, one, 0)

        gone = c + n - OWN_SENT

        @pl.when((n >= OWN_SENT) & (gone < nb))
        def _():
            sent(c, gone, (psem, nxt), (msem, prv))

        npd, npi = plus_next(pd, pi, p)
        nmd, nmi = minus_next(md, mi, p)
        a, b = plus_next(qpd, qpi, q)
        e, f = minus_next(qmd, qmi, q)
        hold = lambda new, was: jnp.where(late, new, was)
        again = n >= lag
        stay = jnp.int32(-1)
        view = [jnp.where(again, x, y) for x, y in zip(old, (old[0], stay, old[2], stay))]
        moved = left_onward(view)
        old = [jnp.where(again, x, y) for x, y in zip(moved, old)]
        return (npd, npi, nmd, nmi, hold(a, qpd), hold(b, qpi), hold(e, qmd), hold(f, qmi), *old)

    one_ = jnp.int32(1)
    mine = (one_, plus_start(1, p), one_, minus_start(1, p))
    other = (one_, plus_start(1, q), one_, minus_start(1, q))
    state = lax.fori_loop(0, SLOTS, step, (*mine, *other, *mine))
    lax.fori_loop(0, lag, lambda n, cur: left_onward(cur), tuple(state[8:]))


def round_kernel(x_ref, o_ref, buf, sem):
    n = sem.shape[0]
    rows = x_ref.shape[0] // n
    step = 64

    def copy(j):
        part = pl.ds(pl.multiple_of(j * rows, rows), rows)
        return pltpu.make_async_copy(buf.at[part, :], o_ref.at[part, :], sem.at[j])

    def one(j, carry):
        def some(m, carry):
            part = pl.ds(pl.multiple_of(j * rows + m * step, step), step)
            buf[part, :] = x_ref[part, :].astype(buf.dtype)
            return carry

        lax.fori_loop(0, rows // step, some, 0)
        copy(j).start()
        return carry

    lax.fori_loop(0, n, one, 0)
    lax.fori_loop(0, n, lambda j, x: (copy(j).wait(), x)[1], 0)


def solution(mesh):
    def local(l_cols, b_cols):
        order, width = b_cols.shape
        nb = order // BLOCK
        tiles = nb * (nb + 1) // 2
        l_cols = pltpu.with_memory_space_constraint(l_cols, pltpu.HBM)
        b_cols = pltpu.with_memory_space_constraint(b_cols, pltpu.HBM)
        acc = pl.pallas_call(
            functools.partial(kernel, nb),
            out_shape=pltpu.VMEM((order, width), jnp.float32),
            in_specs=[pl.BlockSpec(memory_space=pltpu.HBM)] * 2,
            out_specs=pl.BlockSpec(memory_space=pltpu.VMEM),
            scratch_shapes=[
                pltpu.VMEM((tiles, BLOCK, BLOCK), jnp.bfloat16),
                pltpu.VMEM((nb, BLOCK + BLOCK // 2, BLOCK // 2), jnp.bfloat16),
                pltpu.VMEM((order, width), jnp.bfloat16),
                pltpu.SemaphoreType.DMA((tiles,)),
                pltpu.SemaphoreType.DMA((tiles,)),
                pltpu.SemaphoreType.DMA((tiles,)),
                pltpu.SemaphoreType.DMA((tiles,)),
                pltpu.SemaphoreType.DMA((nb,)),
            ],
            compiler_params=pltpu.CompilerParams(
                collective_id=0, has_side_effects=True, vmem_limit_bytes=34 * 2**20),
        )(l_cols, b_cols)
        return pl.pallas_call(
            round_kernel,
            out_shape=jax.ShapeDtypeStruct((order, width), jnp.bfloat16),
            in_specs=[pl.BlockSpec(memory_space=pltpu.VMEM)],
            out_specs=pl.BlockSpec(memory_space=pltpu.HBM),
            scratch_shapes=[
                pltpu.VMEM((order, width), jnp.bfloat16),
                pltpu.SemaphoreType.DMA((16,)),
            ],
            compiler_params=pltpu.CompilerParams(vmem_limit_bytes=16 * 2**20),
        )(acc)

    return jax.shard_map(local, mesh=mesh, in_specs=(P("batch", "col"), P("batch", "col")),
                         out_specs=P("batch", "col"), check_vma=False)
```

time: 116 us -> 109 us (0.940)
  the two profiles are of different devices: /device:TPU:247 before, /device:TPU:253 now
where the time goes in v2:
time: 109 us
  Pallas kernels  109 us (100%)
    pallas_call x1, Pallas kernels, local(): pl.pallas_call(functools.partial(kernel, nb), out_shape=pltpu.VMEM((order...  106 us
    pallas_call x1, Pallas kernels, local(): pl.pallas_call(round_kernel, out_shape=jax.ShapeDtypeStruct((order, width...  3.48 us

profile of v2, /device:TPU:253, one launch (start us, length us, event | category | flops | bytes accessed | tf_op | source)
XLA Modules:
  0.0 109.0 jit_solution(16797338324291740831)
XLA Ops:
  0.0 105.5 %shard_map.28.x_ref = f32[4096,1024]{1,0:T(8,128)S(1)} custom-call(bf16[4096,256]{1,0:T(8,128)(2,1)} %l_ref.1, bf16[4096,1024]{1,0:T(8,128)(2,1)} %b_ref.1), custom_call_target="tpu_custom_call" | custom-call | tf_op jit(solution)/shard_map/pallas_call | solution.py:301
  105.6 3.5 %shard_map.29 = bf16[4096,1024]{1,0:T(8,128)(2,1)} custom-call(f32[4096,1024]{1,0:T(8,128)S(1)} %shard_map.28.x_ref), custom_call_target="tpu_custom_call" | custom-call | tf_op jit(solution)/shard_map/pallas_call | solution.py:319

commit v3 on v2

--- a/solution.py
+++ b/solution.py
@@ -134,7 +134,6 @@
         return pltpu.make_async_copy(l_ref.at[rows, :], lv.at[t], rsem.at[t])
 
     lax.fori_loop(c + 1, nb, lambda i, x: (own_copy(i).start(), x)[1], 0)
-    lax.fori_loop(0, nb, lambda k, x: (b_copy(k).start(), x)[1], 0)
     lax.fori_loop(c, nb, lambda i, x: (land(c, i), x)[1], 0)
     pl.semaphore_wait(barrier, 3)
 
@@ -144,6 +143,7 @@
         return carry
 
     lax.fori_loop(0, nb - c, send_own, 0)
+    lax.fori_loop(0, nb, lambda k, x: (b_copy(k).start(), x)[1], 0)
 
     def clear(i, carry):
         acc[pl.ds(pl.multiple_of(i * 64, 64), 64), :] = jnp.zeros((64, acc.shape[1]), jnp.float32)
@@ -235,13 +235,14 @@
 
                 multiply(k, i)
 
-                @pl.when(j < 3)
-                def _():
-                    sent(k, i, (dsem, mate))
-
             return carry
 
         lax.fori_loop(0, 6, one, 0)
+
+        for k, i in zip(ks[:3], is_[:3]):
+            @pl.when(i >= 0)
+            def _():
+                sent(k, i, (dsem, mate))
 
         gone = c + n - OWN_SENT
 

time: 109 us -> 107 us (0.982)
  the two profiles are of different devices: /device:TPU:253 before, /device:TPU:22 now
where the time goes in v3:
time: 107 us; the launch traced here: 106 us
  Pallas kernels  106 us (99%)
    pallas_call x1, Pallas kernels, local(): pl.pallas_call(functools.partial(kernel, nb), out_shape=pltpu.VMEM((order...  103 us
    pallas_call x1, Pallas kernels, local(): pl.pallas_call(round_kernel, out_shape=jax.ShapeDtypeStruct((order, width...  3.48 us

profile of v3, /device:TPU:22, one launch (start us, length us, event | category | flops | bytes accessed | tf_op | source)
XLA Modules:
  0.0 106.4 jit_solution(1099900326418154857)
XLA Ops:
  0.0 102.9 %shard_map.28.x_ref = f32[4096,1024]{1,0:T(8,128)S(1)} custom-call(bf16[4096,256]{1,0:T(8,128)(2,1)} %l_ref.1, bf16[4096,1024]{1,0:T(8,128)(2,1)} %b_ref.1), custom_call_target="tpu_custom_call" | custom-call | tf_op jit(solution)/shard_map/pallas_call | solution.py:302
  102.9 3.5 %shard_map.29 = bf16[4096,1024]{1,0:T(8,128)(2,1)} custom-call(f32[4096,1024]{1,0:T(8,128)S(1)} %shard_map.28.x_ref), custom_call_target="tpu_custom_call" | custom-call | tf_op jit(solution)/shard_map/pallas_call | solution.py:320

commit v4 on v3

v4 whole, which is shorter than its diff:
```python
import functools

import jax
import jax.numpy as jnp
from jax import lax
from jax.experimental import pallas as pl
from jax.experimental.pallas import tpu as pltpu
from jax.sharding import PartitionSpec as P

BLOCK = 256
MESH = pl.DeviceIdType.MESH
CHIPS = 8
PLUS_HOPS = (2, 2, 3, 5, 4, 4, 3, 2)
LONGER = {(0, 3): 12, (1, 3): 7, (1, 4): 13, (2, 4): 6, (2, 5): 9}
MORE_ODD = (2, 5)
SLOTS = 37
FIRST_SENT = 20


def pick(index, values):
    out = jnp.int32(values[-1])
    for j in range(len(values) - 2, -1, -1):
        out = jnp.where(index == j, jnp.int32(values[j]), out)
    return out


def kernel(nb, l_ref, b_ref, acc, lv, dg, bv, rsem, fsem, dsem, bsem):
    c = lax.axis_index("col")
    z, p = c // 2, c % 2
    q = 1 - p
    mate = z * 2 + q
    ahead = ((z + CHIPS + 2 * p - 1) % CHIPS) * 2 + p
    behind = ((z + CHIPS + 1 - 2 * p) % CHIPS) * 2 + p
    half = BLOCK // 2

    def split(s, d, par):
        t = jnp.where(d <= pick(s, PLUS_HOPS), 0, nb)
        for (s0, d0), v in LONGER.items():
            v = v - par if (s0, d0) == MORE_ODD else v
            t = jnp.where(s * CHIPS + d == s0 * CHIPS + d0, v, t)
        return t

    def source(core, d):
        return (z + CHIPS + (1 - 2 * core) * d) % CHIPS

    def bounds(core, d, par):
        s = source(core, d)
        k = 2 * s + par
        plus = core == 1
        here = split(s, jnp.where(plus, d, CHIPS - d), par)
        on = split(s, jnp.where(plus, d + 1, CHIPS - 1 - d), par)
        low = jnp.where(plus, jnp.maximum(k, here), k)
        high = jnp.where(plus, nb, here)
        on_low = jnp.where(plus, jnp.maximum(k, on), k)
        on_high = jnp.where(plus, nb, on)
        return k, low, high, on_low, on_high

    def inside(i, low, high):
        return (i >= low) & (i < high)

    def ends(core, d):
        _, l0, h0, _, _ = bounds(core, d, 0)
        _, l1, h1, _, _ = bounds(core, d, 1)
        return jnp.minimum(l0, l1), jnp.maximum(h0, h1)

    def start(core, d):
        low, high = ends(core, d)
        return jnp.where(low < high, jnp.where(core == 1, high - 1, low), -1)

    def advance(core, d, i):
        low, high = ends(core, d)
        j = jnp.where(core == 1, i - 1, i + 1)
        more = inside(j, low, high)
        ended = i < 0
        j = jnp.where(more, j, start(core, d + 1))
        return jnp.where(more | ended, d, d + 1), jnp.where(ended, i, j)

    def tiles(core, d, i):
        out = []
        for par in range(2):
            k, low, high, on_low, on_high = bounds(core, d, par)
            out.append((k, jnp.where(inside(i, low, high), i, -1), inside(i, on_low, on_high)))
        return out

    def slot(k, i):
        return nb * k - k * (k - 1) // 2 + i - k

    def each(k, i, fn):
        t = slot(k, i)

        @pl.when(i == k)
        def _():
            fn(dg.at[k], t)

        @pl.when(i != k)
        def _():
            fn(lv.at[t], t)

    def remote(ref, t, sem, dev):
        return pltpu.make_async_remote_copy(
            src_ref=ref, dst_ref=ref, send_sem=sem.at[t], recv_sem=rsem.at[t],
            device_id={"col": dev}, device_id_type=MESH)

    def send(k, i, sem, dev):
        each(k, i, lambda ref, t: remote(ref, t, sem, dev).start())

    def sent(k, i, sem, dev):
        each(k, i, lambda ref, t: remote(ref, t, sem, dev).wait_send())

    def land(k, i):
        each(k, i, lambda ref, t: remote(ref, t, fsem, ahead).wait_recv())

    def b_copy(k):
        rows = pl.ds(pl.multiple_of(k * BLOCK, BLOCK), BLOCK)
        return pltpu.make_async_copy(b_ref.at[rows, :], bv.at[rows, :], bsem.at[k])

    barrier = pltpu.get_barrier_semaphore()
    for dev in (ahead, behind, mate):
        pl.semaphore_signal(barrier, inc=1, device_id={"col": dev}, device_id_type=MESH)

    diag_row = pl.multiple_of(c * BLOCK, BLOCK)
    t_diag = slot(c, c)
    pltpu.make_async_copy(
        l_ref.at[pl.ds(diag_row, BLOCK), pl.ds(0, half)],
        dg.at[c, pl.ds(0, BLOCK), :], rsem.at[t_diag]).start()
    pltpu.make_async_copy(
        l_ref.at[pl.ds(diag_row + half, half), pl.ds(half, half)],
        dg.at[c, pl.ds(BLOCK, half), :], rsem.at[t_diag]).start()

    def own_copy(i):
        rows = pl.ds(pl.multiple_of(i * BLOCK, BLOCK), BLOCK)
        t = slot(c, i)
        return pltpu.make_async_copy(l_ref.at[rows, :], lv.at[t], rsem.at[t])

    lax.fori_loop(c + 1, nb, lambda i, x: (own_copy(i).start(), x)[1], 0)
    lax.fori_loop(c, nb, lambda i, x: (land(c, i), x)[1], 0)
    pl.semaphore_wait(barrier, 3)

    lax.fori_loop(0, nb - c, lambda j, x: (
        send(c, jnp.where(p == 1, c + j, nb - 1 - j), dsem, mate), x)[1], 0)
    lax.fori_loop(0, nb, lambda k, x: (b_copy(k).start(), x)[1], 0)

    def send_first(j, carry):
        i = jnp.where(p == 1, nb - 1 - j, 2 * z + j)

        @pl.when(i >= c)
        def _():
            send(c, i, fsem, ahead)

        @pl.when(i >= mate)
        def _():
            land(mate, i)
            send(mate, i, fsem, ahead)

        return carry

    lax.fori_loop(0, nb - 2 * z, send_first, 0)

    def clear(i, carry):
        acc[pl.ds(pl.multiple_of(i * 64, 64), 64), :] = jnp.zeros((64, acc.shape[1]), jnp.float32)
        return carry

    lax.fori_loop(0, acc.shape[0] // 64, clear, 0)
    lax.fori_loop(0, nb, lambda k, x: (b_copy(k).wait(), x)[1], 0)

    width = acc.shape[1] // 2

    def multiply(k, i):
        row = pl.multiple_of(i * BLOCK, BLOCK)
        depth = pl.multiple_of(k * BLOCK, BLOCK)

        @pl.when(i != k)
        def _():
            tile = lv[slot(k, i)]
            for n in range(2):
                cols = slice(n * width, (n + 1) * width)
                acc[pl.ds(row, BLOCK), cols] += jnp.dot(
                    tile, bv[pl.ds(depth, BLOCK), cols], preferred_element_type=jnp.float32)

        @pl.when(i == k)
        def _():
            left, corner = dg[k, :BLOCK, :], dg[k, BLOCK:, :]
            for n in range(2):
                cols = slice(n * width, (n + 1) * width)
                acc[pl.ds(row, BLOCK), cols] += jnp.dot(
                    left, bv[pl.ds(depth, half), cols], preferred_element_type=jnp.float32)
                acc[pl.ds(row + half, half), cols] += jnp.dot(
                    corner, bv[pl.ds(depth + half, half), cols], preferred_element_type=jnp.float32)

    lag = nb - 2 * z + 3

    def left_onward(d, i):
        for k, _, on in tiles(p, d, i):
            @pl.when(on)
            def _():
                sent(k, i, fsem, ahead)

        return advance(p, d, i)

    def step(n, cur):
        d, i, qd, qi, od, oi = cur
        mine = tiles(p, d, i)
        for k, r, on in mine:
            @pl.when(r >= 0)
            def _():
                land(k, r)

                @pl.when(on)
                def _():
                    send(k, r, fsem, ahead)

                send(k, r, dsem, mate)

        late = n >= 1
        theirs = tiles(q, qd, jnp.where(late, qi, -1))
        own = jnp.where(c + n < nb, c + n, -1)
        other = jnp.where(mate + n < nb, mate + n, -1)
        todo = [x[:2] for x in mine] + [(c, own), (mate, other)] + [x[:2] for x in theirs]

        def one(j, carry):
            k, r = todo[-1]
            for x in range(4, -1, -1):
                k = jnp.where(j == x, todo[x][0], k)
                r = jnp.where(j == x, todo[x][1], r)

            @pl.when(r >= 0)
            def _():
                @pl.when(j >= 4)
                def _():
                    land(k, r)

                multiply(k, r)

            return carry

        lax.fori_loop(0, 6, one, 0)

        for k, r in todo[:3]:
            @pl.when(r >= 0)
            def _():
                sent(k, r, dsem, mate)

        gone = n - FIRST_SENT
        for k in (c, mate):
            @pl.when((gone >= 0) & (k + gone < nb))
            def _():
                sent(k, k + gone, fsem, ahead)

        nd, ni = advance(p, d, i)
        a, b = advance(q, qd, qi)
        again = n >= lag
        e, f = left_onward(od, jnp.where(again, oi, -1))
        hold = lambda cond, new, was: jnp.where(cond, new, was)
        return nd, ni, hold(late, a, qd), hold(late, b, qi), hold(again, e, od), hold(again, f, oi)

    one_ = jnp.int32(1)
    mine = (one_, start(p, one_))
    state = lax.fori_loop(0, SLOTS, step, (*mine, one_, start(q, one_), *mine))
    lax.fori_loop(0, lag, lambda n, cur: left_onward(*cur), tuple(state[4:]))


def round_kernel(x_ref, o_ref, buf, sem):
    n = sem.shape[0]
    rows = x_ref.shape[0] // n
    step = 64

    def copy(j):
        part = pl.ds(pl.multiple_of(j * rows, rows), rows)
        return pltpu.make_async_copy(buf.at[part, :], o_ref.at[part, :], sem.at[j])

    def one(j, carry):
        def some(m, carry):
            part = pl.ds(pl.multiple_of(j * rows + m * step, step), step)
            buf[part, :] = x_ref[part, :].astype(buf.dtype)
            return carry

        lax.fori_loop(0, rows // step, some, 0)
        copy(j).start()
        return carry

    lax.fori_loop(0, n, one, 0)
    lax.fori_loop(0, n, lambda j, x: (copy(j).wait(), x)[1], 0)


def solution(mesh):
    def local(l_cols, b_cols):
        order, width = b_cols.shape
        nb = order // BLOCK
        tiles = nb * (nb + 1) // 2
        l_cols = pltpu.with_memory_space_constraint(l_cols, pltpu.HBM)
        b_cols = pltpu.with_memory_space_constraint(b_cols, pltpu.HBM)
        acc = pl.pallas_call(
            functools.partial(kernel, nb),
            out_shape=pltpu.VMEM((order, width), jnp.float32),
            in_specs=[pl.BlockSpec(memory_space=pltpu.HBM)] * 2,
            out_specs=pl.BlockSpec(memory_space=pltpu.VMEM),
            scratch_shapes=[
                pltpu.VMEM((tiles, BLOCK, BLOCK), jnp.bfloat16),
                pltpu.VMEM((nb, BLOCK + BLOCK // 2, BLOCK // 2), jnp.bfloat16),
                pltpu.VMEM((order, width), jnp.bfloat16),
                pltpu.SemaphoreType.DMA((tiles,)),
                pltpu.SemaphoreType.DMA((tiles,)),
                pltpu.SemaphoreType.DMA((tiles,)),
                pltpu.SemaphoreType.DMA((nb,)),
            ],
            compiler_params=pltpu.CompilerParams(
                collective_id=0, has_side_effects=True, vmem_limit_bytes=34 * 2**20),
        )(l_cols, b_cols)
        return pl.pallas_call(
            round_kernel,
            out_shape=jax.ShapeDtypeStruct((order, width), jnp.bfloat16),
            in_specs=[pl.BlockSpec(memory_space=pltpu.VMEM)],
            out_specs=pl.BlockSpec(memory_space=pltpu.HBM),
            scratch_shapes=[
                pltpu.VMEM((order, width), jnp.bfloat16),
                pltpu.SemaphoreType.DMA((16,)),
            ],
            compiler_params=pltpu.CompilerParams(vmem_limit_bytes=16 * 2**20),
        )(acc)

    return jax.shard_map(local, mesh=mesh, in_specs=(P("batch", "col"), P("batch", "col")),
                         out_specs=P("batch", "col"), check_vma=False)
```

time: 107 us -> 106 us (level)
  no operation moved by 1% of the time
where the time goes in v4:
time: 106 us
  Pallas kernels  106 us (100%)
    pallas_call x1, Pallas kernels, local(): pl.pallas_call(functools.partial(kernel, nb), out_shape=pltpu.VMEM((order...  103 us
    pallas_call x1, Pallas kernels, local(): pl.pallas_call(round_kernel, out_shape=jax.ShapeDtypeStruct((order, width...  3.48 us

profile of v4, /device:TPU:22, one launch (start us, length us, event | category | flops | bytes accessed | tf_op | source)
XLA Modules:
  0.0 106.3 jit_solution(14531962948791594023)
XLA Ops:
  0.0 102.9 %shard_map.28.x_ref = f32[4096,1024]{1,0:T(8,128)S(1)} custom-call(bf16[4096,256]{1,0:T(8,128)(2,1)} %l_ref.1, bf16[4096,1024]{1,0:T(8,128)(2,1)} %b_ref.1), custom_call_target="tpu_custom_call" | custom-call | tf_op jit(solution)/shard_map/pallas_call | solution.py:292
  102.9 3.5 %shard_map.29 = bf16[4096,1024]{1,0:T(8,128)(2,1)} custom-call(f32[4096,1024]{1,0:T(8,128)S(1)} %shard_map.28.x_ref), custom_call_target="tpu_custom_call" | custom-call | tf_op jit(solution)/shard_map/pallas_call | solution.py:309

commit v5 on v4

--- a/solution.py
+++ b/solution.py
@@ -24,7 +24,7 @@
     return out
 
 
-def kernel(nb, l_ref, b_ref, acc, lv, dg, bv, rsem, fsem, dsem, bsem):
+def kernel(nb, l_ref, b_ref, acc, lv, dg, raw, bv, rsem, fsem, dsem, bsem, gsem):
     c = lax.axis_index("col")
     z, p = c // 2, c % 2
     q = 1 - p
@@ -119,13 +119,16 @@
         pl.semaphore_signal(barrier, inc=1, device_id={"col": dev}, device_id_type=MESH)
 
     diag_row = pl.multiple_of(c * BLOCK, BLOCK)
-    t_diag = slot(c, c)
-    pltpu.make_async_copy(
-        l_ref.at[pl.ds(diag_row, BLOCK), pl.ds(0, half)],
-        dg.at[c, pl.ds(0, BLOCK), :], rsem.at[t_diag]).start()
-    pltpu.make_async_copy(
-        l_ref.at[pl.ds(diag_row + half, half), pl.ds(half, half)],
-        dg.at[c, pl.ds(BLOCK, half), :], rsem.at[t_diag]).start()
+    quarter = [
+        pltpu.make_async_copy(l_ref.at[pl.ds(diag_row, half), pl.ds(0, half)], raw.at[0], gsem.at[0]),
+        pltpu.make_async_copy(l_ref.at[pl.ds(diag_row + half, half), pl.ds(half, half)], raw.at[1], gsem.at[1]),
+        pltpu.make_async_copy(
+            l_ref.at[pl.ds(diag_row + half, half), pl.ds(0, half)], dg.at[c, pl.ds(half, half), :], gsem.at[2]),
+    ]
+    for copy in quarter:
+        copy.start()
+    row = lax.broadcasted_iota(jnp.int32, (half, half), 0)
+    col = lax.broadcasted_iota(jnp.int32, (half, half), 1)
 
     def own_copy(i):
         rows = pl.ds(pl.multiple_of(i * BLOCK, BLOCK), BLOCK)
@@ -133,17 +136,24 @@
         return pltpu.make_async_copy(l_ref.at[rows, :], lv.at[t], rsem.at[t])
 
     lax.fori_loop(c + 1, nb, lambda i, x: (own_copy(i).start(), x)[1], 0)
-    lax.fori_loop(c, nb, lambda i, x: (land(c, i), x)[1], 0)
+    for copy in quarter:
+        copy.wait()
+    corner = raw[1].astype(jnp.float32)
+    dg[c, :half, :] = jnp.where(row >= col, raw[0].astype(jnp.float32), corner.T).astype(dg.dtype)
+    line = jnp.sum(jnp.where(row == col, corner, 0.0), axis=0, keepdims=True)
+    dg[c, BLOCK:, :] = jnp.broadcast_to(line, (dg.shape[1] - BLOCK, half)).astype(dg.dtype)
+    lax.fori_loop(c + 1, nb, lambda i, x: (own_copy(i).wait(), x)[1], 0)
+    lax.fori_loop(0, nb, lambda k, x: (b_copy(k).start(), x)[1], 0)
     pl.semaphore_wait(barrier, 3)
 
+    send(c, jnp.where(p == 1, nb - 1, c), fsem, ahead)
     lax.fori_loop(0, nb - c, lambda j, x: (
         send(c, jnp.where(p == 1, c + j, nb - 1 - j), dsem, mate), x)[1], 0)
-    lax.fori_loop(0, nb, lambda k, x: (b_copy(k).start(), x)[1], 0)
 
     def send_first(j, carry):
         i = jnp.where(p == 1, nb - 1 - j, 2 * z + j)
 
-        @pl.when(i >= c)
+        @pl.when((i >= c) & (j > 0))
         def _():
             send(c, i, fsem, ahead)
 
@@ -166,7 +176,7 @@
     width = acc.shape[1] // 2
 
     def multiply(k, i):
-        row = pl.multiple_of(i * BLOCK, BLOCK)
+        at = pl.multiple_of(i * BLOCK, BLOCK)
         depth = pl.multiple_of(k * BLOCK, BLOCK)
 
         @pl.when(i != k)
@@ -174,20 +184,26 @@
             tile = lv[slot(k, i)]
             for n in range(2):
                 cols = slice(n * width, (n + 1) * width)
-                acc[pl.ds(row, BLOCK), cols] += jnp.dot(
+                acc[pl.ds(at, BLOCK), cols] += jnp.dot(
                     tile, bv[pl.ds(depth, BLOCK), cols], preferred_element_type=jnp.float32)
 
         @pl.when(i == k)
         def _():
-            left, corner = dg[k, :BLOCK, :], dg[k, BLOCK:, :]
+            both = dg[k, :half, :].astype(jnp.float32)
+            line = dg[k, BLOCK:BLOCK + 1, :].astype(jnp.float32)
+            top = jnp.where(row >= col, both, 0.0).astype(lv.dtype)
+            left = dg[k, half:BLOCK, :]
+            corner = jnp.where(row < col, both, jnp.where(row == col, line, 0.0)).T.astype(lv.dtype)
             for n in range(2):
                 cols = slice(n * width, (n + 1) * width)
-                acc[pl.ds(row, BLOCK), cols] += jnp.dot(
-                    left, bv[pl.ds(depth, half), cols], preferred_element_type=jnp.float32)
-                acc[pl.ds(row + half, half), cols] += jnp.dot(
-                    corner, bv[pl.ds(depth + half, half), cols], preferred_element_type=jnp.float32)
-
-    lag = nb - 2 * z + 3
+                upper = bv[pl.ds(depth, half), cols]
+                lower = bv[pl.ds(depth + half, half), cols]
+                acc[pl.ds(at, half), cols] += jnp.dot(top, upper, preferred_element_type=jnp.float32)
+                acc[pl.ds(at + half, half), cols] += jnp.dot(
+                    left, upper, preferred_element_type=jnp.float32) + jnp.dot(
+                    corner, lower, preferred_element_type=jnp.float32)
+
+    lag = nb - 2 * z + 2
 
     def left_onward(d, i):
         for k, _, on in tiles(p, d, i):
@@ -296,12 +312,14 @@
             out_specs=pl.BlockSpec(memory_space=pltpu.VMEM),
             scratch_shapes=[
                 pltpu.VMEM((tiles, BLOCK, BLOCK), jnp.bfloat16),
-                pltpu.VMEM((nb, BLOCK + BLOCK // 2, BLOCK // 2), jnp.bfloat16),
+                pltpu.VMEM((nb, BLOCK + 16, BLOCK // 2), jnp.bfloat16),
+                pltpu.VMEM((2, BLOCK // 2, BLOCK // 2), jnp.bfloat16),
                 pltpu.VMEM((order, width), jnp.bfloat16),
                 pltpu.SemaphoreType.DMA((tiles,)),
                 pltpu.SemaphoreType.DMA((tiles,)),
                 pltpu.SemaphoreType.DMA((tiles,)),
                 pltpu.SemaphoreType.DMA((nb,)),
+                pltpu.SemaphoreType.DMA((3,)),
             ],
             compiler_params=pltpu.CompilerParams(
                 collective_id=0, has_side_effects=True, vmem_limit_bytes=34 * 2**20),

time: 106 us -> 105 us (level)
  Pallas kernels: 106 us -> 104 us
    pallas_call x1, Pallas kernels: 103 us -> 101 us  [local(): pl.pallas_call(functools.partial(kernel, nb), out_shape=pltpu.VMEM((order...]
where the time goes in v5:
time: 105 us; the launch traced here: 104 us
  Pallas kernels  104 us (99%)
    pallas_call x1, Pallas kernels, local(): pl.pallas_call(functools.partial(kernel, nb), out_shape=pltpu.VMEM((order...  101 us
    pallas_call x1, Pallas kernels, local(): pl.pallas_call(round_kernel, out_shape=jax.ShapeDtypeStruct((order, width...  3.48 us

profile of v5, /device:TPU:22, one launch (start us, length us, event | category | flops | bytes accessed | tf_op | source)
XLA Modules:
  0.0 104.4 jit_solution(12901823846800999658)
XLA Ops:
  0.0 100.9 %shard_map.28.x_ref = f32[4096,1024]{1,0:T(8,128)S(1)} custom-call(bf16[4096,256]{1,0:T(8,128)(2,1)} %l_ref.1, bf16[4096,1024]{1,0:T(8,128)(2,1)} %b_ref.1), custom_call_target="tpu_custom_call" | custom-call | tf_op jit(solution)/shard_map/pallas_call | solution.py:308
  100.9 3.5 %shard_map.29 = bf16[4096,1024]{1,0:T(8,128)(2,1)} custom-call(f32[4096,1024]{1,0:T(8,128)S(1)} %shard_map.28.x_ref), custom_call_target="tpu_custom_call" | custom-call | tf_op jit(solution)/shard_map/pallas_call | solution.py:327

commit v6 on v5

--- a/solution.py
+++ b/solution.py
@@ -13,8 +13,9 @@
 PLUS_HOPS = (2, 2, 3, 5, 4, 4, 3, 2)
 LONGER = {(0, 3): 12, (1, 3): 7, (1, 4): 13, (2, 4): 6, (2, 5): 9}
 MORE_ODD = (2, 5)
-SLOTS = 37
-FIRST_SENT = 20
+SLOTS = 36
+RING = 19
+LAPS = 4
 
 
 def pick(index, values):
@@ -24,14 +25,15 @@
     return out
 
 
-def kernel(nb, l_ref, b_ref, acc, lv, dg, raw, bv, rsem, fsem, dsem, bsem, gsem):
+def kernel(nb, l_ref, b_ref, acc, lv, dg, raw, bv, isem, osem, xsem, fsem, dsem, bsem, credit):
     c = lax.axis_index("col")
     z, p = c // 2, c % 2
     q = 1 - p
     mate = z * 2 + q
-    ahead = ((z + CHIPS + 2 * p - 1) % CHIPS) * 2 + p
-    behind = ((z + CHIPS + 1 - 2 * p) % CHIPS) * 2 + p
+    ahead = ((z + CHIPS + 1 - 2 * p) % CHIPS) * 2 + p
+    behind = ((z + CHIPS + 2 * p - 1) % CHIPS) * 2 + p
     half = BLOCK // 2
+    first_slots = nb - 2 * z
 
     def split(s, d, par):
         t = jnp.where(d <= pick(s, PLUS_HOPS), 0, nb)
@@ -41,12 +43,12 @@
         return t
 
     def source(core, d):
-        return (z + CHIPS + (1 - 2 * core) * d) % CHIPS
+        return (z + CHIPS + (2 * core - 1) * d) % CHIPS
 
     def bounds(core, d, par):
         s = source(core, d)
         k = 2 * s + par
-        plus = core == 1
+        plus = core == 0
         here = split(s, jnp.where(plus, d, CHIPS - d), par)
         on = split(s, jnp.where(plus, d + 1, CHIPS - 1 - d), par)
         low = jnp.where(plus, jnp.maximum(k, here), k)
@@ -65,11 +67,11 @@
 
     def start(core, d):
         low, high = ends(core, d)
-        return jnp.where(low < high, jnp.where(core == 1, high - 1, low), -1)
+        return jnp.where(low < high, jnp.where(core == 0, high - 1, low), -1)
 
     def advance(core, d, i):
         low, high = ends(core, d)
-        j = jnp.where(core == 1, i - 1, i + 1)
+        j = jnp.where(core == 0, i - 1, i + 1)
         more = inside(j, low, high)
         ended = i < 0
         j = jnp.where(more, j, start(core, d + 1))
@@ -79,40 +81,37 @@
         out = []
         for par in range(2):
             k, low, high, on_low, on_high = bounds(core, d, par)
-            out.append((k, jnp.where(inside(i, low, high), i, -1), inside(i, on_low, on_high)))
+            out.append((k, inside(i, low, high), inside(i, on_low, on_high)))
         return out
 
     def slot(k, i):
         return nb * k - k * (k - 1) // 2 + i - k
 
     def each(k, i, fn):
-        t = slot(k, i)
-
         @pl.when(i == k)
         def _():
-            fn(dg.at[k], t)
+            fn(dg.at[k])
 
         @pl.when(i != k)
         def _():
-            fn(lv.at[t], t)
-
-    def remote(ref, t, sem, dev):
+            fn(lv.at[slot(k, i)])
+
+    def remote(ref, out, arrive, dev):
         return pltpu.make_async_remote_copy(
-            src_ref=ref, dst_ref=ref, send_sem=sem.at[t], recv_sem=rsem.at[t],
+            src_ref=ref, dst_ref=ref, send_sem=out, recv_sem=arrive,
             device_id={"col": dev}, device_id_type=MESH)
 
-    def send(k, i, sem, dev):
-        each(k, i, lambda ref, t: remote(ref, t, sem, dev).start())
-
-    def sent(k, i, sem, dev):
-        each(k, i, lambda ref, t: remote(ref, t, sem, dev).wait_send())
-
-    def land(k, i):
-        each(k, i, lambda ref, t: remote(ref, t, fsem, ahead).wait_recv())
-
-    def b_copy(k):
-        rows = pl.ds(pl.multiple_of(k * BLOCK, BLOCK), BLOCK)
-        return pltpu.make_async_copy(b_ref.at[rows, :], bv.at[rows, :], bsem.at[k])
+    def send(k, i, out, arrive, dev):
+        each(k, i, lambda ref: remote(ref, out, arrive, dev).start())
+
+    def sent(k, i, out, dev):
+        each(k, i, lambda ref: remote(ref, out, isem.at[0], dev).wait_send())
+
+    def land(k, i, arrive):
+        each(k, i, lambda ref: remote(ref, fsem.at[0], arrive, ahead).wait_recv())
+
+    def out_sem(m, par):
+        return fsem.at[(m % RING) * 2 + par]
 
     barrier = pltpu.get_barrier_semaphore()
     for dev in (ahead, behind, mate):
@@ -120,10 +119,10 @@
 
     diag_row = pl.multiple_of(c * BLOCK, BLOCK)
     quarter = [
-        pltpu.make_async_copy(l_ref.at[pl.ds(diag_row, half), pl.ds(0, half)], raw.at[0], gsem.at[0]),
-        pltpu.make_async_copy(l_ref.at[pl.ds(diag_row + half, half), pl.ds(half, half)], raw.at[1], gsem.at[1]),
+        pltpu.make_async_copy(l_ref.at[pl.ds(diag_row, half), pl.ds(0, half)], raw.at[0], fsem.at[0]),
+        pltpu.make_async_copy(l_ref.at[pl.ds(diag_row + half, half), pl.ds(half, half)], raw.at[1], fsem.at[1]),
         pltpu.make_async_copy(
-            l_ref.at[pl.ds(diag_row + half, half), pl.ds(0, half)], dg.at[c, pl.ds(half, half), :], gsem.at[2]),
+            l_ref.at[pl.ds(diag_row + half, half), pl.ds(0, half)], dg.at[c, pl.ds(half, half), :], fsem.at[2]),
     ]
     for copy in quarter:
         copy.start()
@@ -132,8 +131,11 @@
 
     def own_copy(i):
         rows = pl.ds(pl.multiple_of(i * BLOCK, BLOCK), BLOCK)
-        t = slot(c, i)
-        return pltpu.make_async_copy(l_ref.at[rows, :], lv.at[t], rsem.at[t])
+        return pltpu.make_async_copy(l_ref.at[rows, :], lv.at[slot(c, i)], dsem.at[i])
+
+    def b_copy(k):
+        rows = pl.ds(pl.multiple_of(k * BLOCK, BLOCK), BLOCK)
+        return pltpu.make_async_copy(b_ref.at[rows, :], bv.at[rows, :], bsem)
 
     lax.fori_loop(c + 1, nb, lambda i, x: (own_copy(i).start(), x)[1], 0)
     for copy in quarter:
@@ -146,34 +148,49 @@
     lax.fori_loop(0, nb, lambda k, x: (b_copy(k).start(), x)[1], 0)
     pl.semaphore_wait(barrier, 3)
 
-    send(c, jnp.where(p == 1, nb - 1, c), fsem, ahead)
-    lax.fori_loop(0, nb - c, lambda j, x: (
-        send(c, jnp.where(p == 1, c + j, nb - 1 - j), dsem, mate), x)[1], 0)
+    head = p
+    send(c, jnp.where(p == 0, nb - 1, c), out_sem(head, p), isem.at[head * 2 + p], ahead)
+    def to_mate(j, carry):
+        i = jnp.where(p == 0, c + j, nb - 1 - j)
+        send(c, i, dsem.at[i], osem.at[i], mate)
+        return carry
+
+    lax.fori_loop(0, nb - c, to_mate, 0)
 
     def send_first(j, carry):
-        i = jnp.where(p == 1, nb - 1 - j, 2 * z + j)
-
-        @pl.when((i >= c) & (j > 0))
-        def _():
-            send(c, i, fsem, ahead)
+        i = jnp.where(p == 0, nb - 1 - j, 2 * z + j)
+
+        @pl.when((i >= c) & (j != head))
+        def _():
+            send(c, i, out_sem(j, p), isem.at[j * 2 + p], ahead)
 
         @pl.when(i >= mate)
         def _():
-            land(mate, i)
-            send(mate, i, fsem, ahead)
+            land(mate, i, osem.at[i])
+            send(mate, i, out_sem(j, q), isem.at[j * 2 + q], ahead)
 
         return carry
 
-    lax.fori_loop(0, nb - 2 * z, send_first, 0)
+    lax.fori_loop(0, first_slots, send_first, 0)
 
     def clear(i, carry):
         acc[pl.ds(pl.multiple_of(i * 64, 64), 64), :] = jnp.zeros((64, acc.shape[1]), jnp.float32)
         return carry
 
     lax.fori_loop(0, acc.shape[0] // 64, clear, 0)
-    lax.fori_loop(0, nb, lambda k, x: (b_copy(k).wait(), x)[1], 0)
+    pltpu.make_async_copy(b_ref, bv, bsem).wait()
 
     width = acc.shape[1] // 2
+
+    def pair(k, i):
+        at = pl.multiple_of(i * BLOCK, BLOCK)
+        depth = pl.multiple_of(k * BLOCK, BLOCK)
+        left, right = lv[slot(k, i)], lv[slot(k + 1, i)]
+        for n in range(2):
+            cols = slice(n * width, (n + 1) * width)
+            acc[pl.ds(at, BLOCK), cols] += jnp.dot(
+                left, bv[pl.ds(depth, BLOCK), cols], preferred_element_type=jnp.float32) + jnp.dot(
+                right, bv[pl.ds(depth + BLOCK, BLOCK), cols], preferred_element_type=jnp.float32)
 
     def multiply(k, i):
         at = pl.multiple_of(i * BLOCK, BLOCK)
@@ -203,76 +220,102 @@
                     left, upper, preferred_element_type=jnp.float32) + jnp.dot(
                     corner, lower, preferred_element_type=jnp.float32)
 
-    lag = nb - 2 * z + 2
-
-    def left_onward(d, i):
-        for k, _, on in tiles(p, d, i):
+    def left_onward(m, d, i):
+        for par, (k, _, on) in enumerate(tiles(p, d, i)):
             @pl.when(on)
             def _():
-                sent(k, i, fsem, ahead)
+                sent(k, i, out_sem(m, par), ahead)
 
         return advance(p, d, i)
 
     def step(n, cur):
-        d, i, qd, qi, od, oi = cur
+        d, i, qd, qi, od, oi, gone = cur
         mine = tiles(p, d, i)
-        for k, r, on in mine:
-            @pl.when(r >= 0)
-            def _():
-                land(k, r)
+        lap = (n % LAPS) * 2
+
+        @pl.when(n >= LAPS)
+        def _():
+            pl.semaphore_wait(credit, 1)
+
+        for par, (k, here, on) in enumerate(mine):
+            @pl.when(here)
+            def _():
+                land(k, i, isem.at[n * 2 + par])
 
                 @pl.when(on)
                 def _():
-                    send(k, r, fsem, ahead)
-
-                send(k, r, dsem, mate)
-
-        late = n >= 1
-        theirs = tiles(q, qd, jnp.where(late, qi, -1))
-        own = jnp.where(c + n < nb, c + n, -1)
-        other = jnp.where(mate + n < nb, mate + n, -1)
-        todo = [x[:2] for x in mine] + [(c, own), (mate, other)] + [x[:2] for x in theirs]
+                    send(k, i, out_sem(first_slots + n, par), isem.at[gone * 2 + par], ahead)
+
+                send(k, i, dsem.at[nb + par], xsem.at[lap + par], mate)
+
+        theirs = tiles(q, qd, qi)
+        at_home = 2 * z + n
+        home = [(2 * z + par, (at_home >= 2 * z + par) & (at_home < nb)) for par in range(2)]
+        groups = (
+            (mine[0][0], i, mine[0][1], mine[1][1]),
+            (home[0][0], at_home, home[0][1], home[1][1]),
+            (theirs[0][0], qi, theirs[0][1], theirs[1][1]),
+        )
 
         def one(j, carry):
-            k, r = todo[-1]
-            for x in range(4, -1, -1):
-                k = jnp.where(j == x, todo[x][0], k)
-                r = jnp.where(j == x, todo[x][1], r)
-
-            @pl.when(r >= 0)
-            def _():
-                @pl.when(j >= 4)
+            k, r, v0, v1 = (
+                jnp.where(j == 0, x, jnp.where(j == 1, y, w))
+                for x, y, w in zip(*[(g[0], g[1], g[2].astype(jnp.int32), g[3].astype(jnp.int32)) for g in groups]))
+            v0, v1 = v0 > 0, v1 > 0
+            for par, v in enumerate((v0, v1)):
+                @pl.when(v & (j == 2))
                 def _():
-                    land(k, r)
-
-                multiply(k, r)
+                    land(k + par, r, xsem.at[lap + par])
+
+            double = v0 & v1 & (r > k + 1)
+
+            @pl.when(double)
+            def _():
+                pair(k, r)
+
+            @pl.when(jnp.logical_not(double))
+            def _():
+                def single(par, carry):
+                    @pl.when(jnp.where(par == 0, v0.astype(jnp.int32), v1.astype(jnp.int32)) > 0)
+                    def _():
+                        multiply(k + par, r)
+
+                    return carry
+
+                lax.fori_loop(0, 2, single, 0)
 
             return carry
 
-        lax.fori_loop(0, 6, one, 0)
-
-        for k, r in todo[:3]:
-            @pl.when(r >= 0)
-            def _():
-                sent(k, r, dsem, mate)
-
-        gone = n - FIRST_SENT
-        for k in (c, mate):
-            @pl.when((gone >= 0) & (k + gone < nb))
-            def _():
-                sent(k, k + gone, fsem, ahead)
-
-        nd, ni = advance(p, d, i)
-        a, b = advance(q, qd, qi)
-        again = n >= lag
-        e, f = left_onward(od, jnp.where(again, oi, -1))
-        hold = lambda cond, new, was: jnp.where(cond, new, was)
-        return nd, ni, hold(late, a, qd), hold(late, b, qi), hold(again, e, od), hold(again, f, oi)
-
-    one_ = jnp.int32(1)
-    mine = (one_, start(p, one_))
-    state = lax.fori_loop(0, SLOTS, step, (*mine, one_, start(q, one_), *mine))
-    lax.fori_loop(0, lag, lambda n, cur: left_onward(*cur), tuple(state[4:]))
+        lax.fori_loop(0, 3, one, 0)
+
+        @pl.when(n < SLOTS - LAPS)
+        def _():
+            pl.semaphore_signal(credit, inc=1, device_id={"col": mate}, device_id_type=MESH)
+
+        for par, (k, here, _) in enumerate(mine):
+            @pl.when(here)
+            def _():
+                sent(k, i, dsem.at[nb + par], mate)
+
+        @pl.when((at_home >= c) & (at_home < nb))
+        def _():
+            sent(c, at_home, dsem.at[at_home], mate)
+
+        again = n >= 2
+        e, f = left_onward(jnp.maximum(n - 2, 0), od, jnp.where(again, oi, -1))
+        gone = gone + (mine[0][2] | mine[1][2]).astype(jnp.int32)
+        return (*advance(p, d, i), *advance(q, qd, qi), jnp.where(again, e, od), jnp.where(again, f, oi), gone)
+
+    zero, one_ = jnp.int32(0), jnp.int32(1)
+    state = lax.fori_loop(0, SLOTS, step, (
+        one_, start(p, one_), one_, start(q, one_), zero, start(p, zero), first_slots))
+    od, oi = state[4:6]
+    left = zero
+    for ahead_d in range(2):
+        for par in range(2):
+            _, _, _, on_low, on_high = bounds(p, od + ahead_d, par)
+            left = jnp.where((oi >= 0) & (on_low < on_high), first_slots + 2, left)
+    lax.fori_loop(0, left, lambda m, cur: left_onward(SLOTS - 2 + m, *cur), (od, oi))
 
 
 def round_kernel(x_ref, o_ref, buf, sem):
@@ -315,11 +358,13 @@
                 pltpu.VMEM((nb, BLOCK + 16, BLOCK // 2), jnp.bfloat16),
                 pltpu.VMEM((2, BLOCK // 2, BLOCK // 2), jnp.bfloat16),
                 pltpu.VMEM((order, width), jnp.bfloat16),
-                pltpu.SemaphoreType.DMA((tiles,)),
-                pltpu.SemaphoreType.DMA((tiles,)),
-                pltpu.SemaphoreType.DMA((tiles,)),
+                pltpu.SemaphoreType.DMA((2 * SLOTS,)),
                 pltpu.SemaphoreType.DMA((nb,)),
-                pltpu.SemaphoreType.DMA((3,)),
+                pltpu.SemaphoreType.DMA((2 * LAPS,)),
+                pltpu.SemaphoreType.DMA((2 * RING,)),
+                pltpu.SemaphoreType.DMA((nb + 2,)),
+                pltpu.SemaphoreType.DMA,
+                pltpu.SemaphoreType.REGULAR,
             ],
             compiler_params=pltpu.CompilerParams(
                 collective_id=0, has_side_effects=True, vmem_limit_bytes=34 * 2**20),

time: 105 us -> 103 us (0.981)
  the two profiles are of different devices: /device:TPU:22 before, /device:TPU:21 now
where the time goes in v6:
time: 103 us
  Pallas kernels  103 us (100%)
    pallas_call x1, Pallas kernels, local(): pl.pallas_call(functools.partial(kernel, nb), out_shape=pltpu.VMEM((order...  99.3 us
    pallas_call x1, Pallas kernels, local(): pl.pallas_call(round_kernel, out_shape=jax.ShapeDtypeStruct((order, width...  3.48 us

profile of v6, /device:TPU:21, one launch (start us, length us, event | category | flops | bytes accessed | tf_op | source)
XLA Modules:
  0.0 102.8 jit_solution(12125167682604813161)
XLA Ops:
  0.0 99.3 %shard_map.28.x_ref = f32[4096,1024]{1,0:T(8,128)S(1)} custom-call(bf16[4096,256]{1,0:T(8,128)(2,1)} %l_ref.1, bf16[4096,1024]{1,0:T(8,128)(2,1)} %b_ref.1), custom_call_target="tpu_custom_call" | custom-call | tf_op jit(solution)/shard_map/pallas_call | solution.py:351
  99.3 3.5 %shard_map.29 = bf16[4096,1024]{1,0:T(8,128)(2,1)} custom-call(f32[4096,1024]{1,0:T(8,128)S(1)} %shard_map.28.x_ref), custom_call_target="tpu_custom_call" | custom-call | tf_op jit(solution)/shard_map/pallas_call | solution.py:372
